TPU v7x, 32 devices: a whole 2x2x4 slice. The times are simulated.
32 devices in a mesh: ctx: 16 (over z, y, x), tp: 2 (over core).
Axes of the slice: x: 2, y: 2, z: 4, core: 2. Of those that a mesh axis runs over, the one named last changes fastest.
Arguments:
- byte_states: bfloat16 [4096, 1024], P('ctx'), may hold values from -12 to 12, as said below
- patch_of_byte: int32 [4096], P('ctx'), may hold values from 0 to 125, as said below
- patch_first: int32 [16], replicated, may hold values from 0 to 991, as said below
- moved: int32 [2, 16], replicated, may hold values from 0 to 32, as said below
- w_qkv: bfloat16 [3, 1024, 2048], P(None, None, 'tp'), may hold values from -0.25 to 0.25, as said below
- d_attn: bfloat16 [1024, 2048], P('ctx', 'tp'), may hold values from -6 to 6
Outputs:
- attn_out: bfloat16 [1024, 2048], P('ctx', 'tp')
- byte_grad: bfloat16 [4096, 1024], P('ctx', 'tp')
Inputs may be any that keep to these rules, and one draw needn't show every extreme that they name: `patch_of_byte`: within each byte shard the numbers start at 0 and rise by 0 or 1 from byte to byte; a shard holds at most 126 patches, reached on some shard. `patch_first`: the sum of the patch counts of all earlier byte shards; shard 0 starts at 0. moved[0, 0] = 0 and moved[1, 15] = 0; every other entry is 1 to 32; every patch shard thereby receives exactly 64 patches, and the patch counts agree with patch_first and patch_of_byte. `w_qkv`: independent entries of order 1024 ** -0.5. `byte_states`: entries of order one.
All inputs are finite; a program needn't handle non-finite values.
Results may differ from a plain program's by a relative error of at most 0.011.
Values may be sent and summed in bfloat16 or wider, within the bound.
A program may use at most 64 MiB of HBM per device.

v0:
```python
import jax
import jax.numpy as jnp
from jax import lax
from jax.sharding import PartitionSpec as P

HD = 128


def extended_2(x, sides, width):
    for axis, dim in sides:
        peers, length = (lax.axis_size(axis), x.shape[dim])
        up = [(i, (i + 1) % peers) for i in range(peers - 1)]
        down = [(j, i) for i, j in up]
        last = lax.slice_in_dim(x, length - width, length, axis=dim)
        first = lax.slice_in_dim(x, 0, width, axis=dim)
        before = lax.ppermute(last, axis, up)
        after = lax.ppermute(first, axis, down)
        x = jnp.concatenate([before, x, after], axis=dim)
    return x


def pick_own(values, index):
    return lax.dynamic_index_in_dim(values, index, 0, keepdims=False)


def shards(byte_states, patch_of_byte, patch_first, moved, w_qkv, d_attn):
    ctx_index = lax.axis_index("ctx")
    n_ctx = lax.axis_size("ctx")
    rows = d_attn.shape[0]
    feats = d_attn.shape[1]
    heads = feats // HD
    capacity = 2 * rows
    total = rows * n_ctx
    scale = HD ** (-0.5)
    ends = jnp.concatenate([patch_first[1:], jnp.full((1,), total, jnp.int32)])
    counts = ends - patch_first
    lower_moves = moved[0]
    upper_moves = moved[1]
    zero_one = jnp.zeros((1,), jnp.int32)
    below_high = jnp.concatenate([zero_one, upper_moves[:-1]])
    above_low = jnp.concatenate([lower_moves[1:], zero_one])
    prev_first = jnp.concatenate([zero_one, patch_first[:-1]])
    prev_count = jnp.concatenate([zero_one, counts[:-1]])
    ranks = jnp.arange(rows, dtype=jnp.int32)[None, :]
    from_low = ranks < below_high[:, None]
    from_high = ranks >= (rows - above_low)[:, None]
    lower_local = prev_count[:, None] - below_high[:, None] + ranks
    own_local = lower_moves[:, None] + ranks - below_high[:, None]
    upper_local = ranks - (rows - above_low)[:, None]
    ids_all = jnp.where(
        from_low,
        prev_first[:, None] + lower_local,
        jnp.where(from_high, ends[:, None] + upper_local, patch_first[:, None] + own_local),
    )
    source_all = jnp.where(
        from_low,
        lower_local,
        jnp.where(from_high, 2 * capacity + upper_local, capacity + own_local),
    )
    wanted = pick_own(ids_all, ctx_index)
    source_rows = pick_own(source_all, ctx_index)
    key_place = ids_all.reshape(-1)
    slots = jnp.arange(capacity, dtype=jnp.int32)
    member = patch_of_byte[None, :] == slots[:, None]
    lengths = jnp.sum(member.astype(jnp.float32), axis=1)
    onehot = member.astype(jnp.bfloat16)
    part = byte_states.shape[1] // lax.axis_size("tp")
    source = lax.dynamic_slice_in_dim(byte_states, lax.axis_index("tp") * part, part, 1)
    pooled_local = (
        jnp.dot(onehot, source, preferred_element_type=jnp.float32)
        / jnp.maximum(lengths, 1.0)[:, None]
    ).astype(jnp.bfloat16)
    extended = extended_2(pooled_local, (("ctx", 0),), capacity)
    picker = (source_rows[:, None] == jnp.arange(3 * capacity, dtype=jnp.int32)[None, :]).astype(
        jnp.bfloat16
    )
    pooled = jnp.dot(picker, extended, preferred_element_type=jnp.float32).astype(jnp.bfloat16)
    pooled = lax.all_gather(pooled, "tp", axis=1, tiled=True)
    query = jnp.dot(pooled, w_qkv[0], preferred_element_type=jnp.float32).astype(jnp.bfloat16)
    keyed = jnp.dot(pooled, w_qkv[1], preferred_element_type=jnp.float32).astype(jnp.bfloat16)
    valued = jnp.dot(pooled, w_qkv[2], preferred_element_type=jnp.float32).astype(jnp.bfloat16)
    keys_all, values_all = (
        lax.all_gather(keyed, "ctx", axis=0, tiled=True),
        lax.all_gather(valued, "ctx", axis=0, tiled=True),
    )
    query3 = query.reshape(rows, heads, HD)
    keys3 = keys_all.reshape(total, heads, HD)
    values3 = values_all.reshape(total, heads, HD)
    causal = (wanted[:, None] >= key_place[None, :])[None, :, :]
    score = jnp.einsum("qhd,khd->hqk", query3, keys3, preferred_element_type=jnp.float32) * scale
    masked = jnp.where(causal, score, -jnp.inf)
    top = jnp.max(masked, axis=2, keepdims=True)
    lse = top + jnp.log(jnp.sum(jnp.exp(masked - top), axis=2, keepdims=True))
    prob = jnp.exp(jnp.where(causal, score - lse, -jnp.inf))
    probs = prob.astype(jnp.bfloat16)
    output3 = jnp.einsum("hqk,khd->qhd", probs, values3, preferred_element_type=jnp.float32).astype(
        jnp.bfloat16
    )
    attn_out = output3.reshape(rows, feats)
    grad3 = d_attn.reshape(rows, heads, HD)
    delta = jnp.sum(grad3.astype(jnp.float32) * output3.astype(jnp.float32), axis=2)
    dprob = jnp.einsum("qhd,khd->hqk", grad3, values3, preferred_element_type=jnp.float32)
    dscore = (prob * (dprob - jnp.transpose(delta)[:, :, None])).astype(jnp.bfloat16)
    d_query = (
        jnp.einsum("hqk,khd->qhd", dscore, keys3, preferred_element_type=jnp.float32) * scale
    ).astype(jnp.bfloat16)
    lse_rows = jnp.transpose(lse[:, :, 0])
    lse_all, delta_all = (
        lax.all_gather(lse_rows, "ctx", axis=0, tiled=True),
        lax.all_gather(delta, "ctx", axis=0, tiled=True),
    )
    own_keys = keyed.reshape(rows, heads, HD)
    own_values = valued.reshape(rows, heads, HD)
    q_piece = lax.all_gather(query, "ctx", axis=0, tiled=True)
    g_piece = lax.all_gather(d_attn, "ctx", axis=0, tiled=True)
    count = q_piece.shape[0]
    q_three = q_piece.reshape(count, heads, HD)
    g_three = g_piece.reshape(count, heads, HD)
    lse_piece = jnp.transpose(lse_all)
    delta_piece = jnp.transpose(delta_all)
    allowed = (key_place[:, None] >= wanted[None, :])[None, :, :]
    part_score = (
        jnp.einsum("qhd,khd->hqk", q_three, own_keys, preferred_element_type=jnp.float32) * scale
    )
    part_prob = jnp.exp(jnp.where(allowed, part_score - lse_piece[:, :, None], -jnp.inf))
    part_probs = part_prob.astype(jnp.bfloat16)
    d_value_sum = jnp.einsum(
        "hqk,qhd->khd", part_probs, g_three, preferred_element_type=jnp.float32
    )
    part_dprob = jnp.einsum("qhd,khd->hqk", g_three, own_values, preferred_element_type=jnp.float32)
    part_dscore = (part_prob * (part_dprob - delta_piece[:, :, None])).astype(jnp.bfloat16)
    d_key_sum = (
        jnp.einsum("hqk,qhd->khd", part_dscore, q_three, preferred_element_type=jnp.float32) * scale
    )
    d_key_sum, d_value_sum = (d_key_sum, d_value_sum)
    d_key = d_key_sum.astype(jnp.bfloat16).reshape(rows, feats)
    d_value = d_value_sum.astype(jnp.bfloat16).reshape(rows, feats)
    d_query = d_query.reshape(rows, feats)
    contract = (((1,), (1,)), ((), ()))
    partial_value = lax.dot_general(d_query, w_qkv[0], contract, preferred_element_type=jnp.float32)
    partial_value = partial_value + lax.dot_general(
        d_key, w_qkv[1], contract, preferred_element_type=jnp.float32
    )
    partial_value = partial_value + lax.dot_general(
        d_value, w_qkv[2], contract, preferred_element_type=jnp.float32
    )
    d_pooled = lax.psum_scatter(partial_value, "tp", scatter_dimension=1, tiled=True).astype(
        jnp.bfloat16
    )
    returned = extended_2(d_pooled, (("ctx", 0),), rows)
    my_count = pick_own(counts, ctx_index)
    my_low = pick_own(lower_moves, ctx_index)
    my_high = pick_own(upper_moves, ctx_index)
    my_below = pick_own(below_high, ctx_index)
    target = jnp.where(
        patch_of_byte < my_low,
        rows - my_low + patch_of_byte,
        jnp.where(
            patch_of_byte >= my_count - my_high,
            2 * rows + patch_of_byte - (my_count - my_high),
            rows + my_below + patch_of_byte - my_low,
        ),
    )
    chooser = (target[:, None] == jnp.arange(3 * rows, dtype=jnp.int32)[None, :]).astype(
        jnp.bfloat16
    )
    spread_back = jnp.dot(chooser, returned, preferred_element_type=jnp.float32)
    byte_lengths = jnp.sum(jnp.where(member, lengths[:, None], 0.0), axis=0)
    byte_grad = (spread_back / byte_lengths[:, None]).astype(jnp.bfloat16)
    return (attn_out, byte_grad)


def solution(mesh):
    placed = (P("ctx", None), P("ctx"), P(), P(), P(None, None, "tp"), P("ctx", "tp"))
    return jax.shard_map(
        shards,
        mesh=mesh,
        in_specs=placed,
        out_specs=(P("ctx", "tp"), P("ctx", "tp")),
        check_vma=False,
    )
```

profile of v0, /device:TPU:0, one launch (start us, length us, event | category | flops | bytes accessed | tf_op | source)
XLA Modules:
  0.0 305.5 jit_solution(10949627991634043434)
XLA Ops:
  9.7 4.9 %collective-permute-start = (bf16[128,512]{1,0:T(8,128)(2,1)S(1)}, bf16[128,512]{1,0:T(8,128)(2,1)S(1)}, u32[]{:S(2)}, u32[]{:S(2)}) collective-permute-start(bf16[128,512]{1,0:T(8,128)(2,1)S(1)} %fusion.56), channel_id=1, source_target_pairs={{0,2},{2,4},{4,6},{6,8},{8,10},{10,12},{12,14},{14,16},{16,18},{18... | collective-permute-start | bytes 393224 | tf_op jit(solution)/shard_map/ppermute | solution.py:16
  21.9 1.9 select_bitcast_fusion
  24.1 1.9 all_gather.21
  26.0 2.7 fusion.66
  28.8 2.7 fusion.60
  31.6 2.7 fusion.63
  35.7 38.1 %all-gather.13.cloned.1.call-done = bf16[1024,1024]{1,0:T(8,128)(2,1)} async-done(((bf16[64,1024]{1,0:T(8,128)(2,1)}), bf16[1024,1024]{1,0:T(8,128)(2,1)}) %all-gather.13.cloned.1.call-update) | async-done | bytes 2097168 | tf_op jit(solution)/shard_map/all_gather | solution.py:115
  73.9 2.9 copy.61
  76.8 59.7 %all-gather.9.cloned.1.call-done = bf16[1024,1024]{1,0:T(8,128)(2,1)} async-done(((bf16[64,1024]{1,0:T(8,128)(2,1)}), bf16[1024,1024]{1,0:T(8,128)(2,1)}) %all-gather.9.cloned.1.call-update) | async-done | bytes 2097168 | tf_op jit(solution)/shard_map/all_gather | solution.py:83
  136.4 2.6 select_reduce_fusion
  141.0 38.9 %all-gather = f32[16,64,8]{1,2,0:T(8,128)S(1)} all-gather(f32[1,64,8]{1,2,0:T(8,128)S(1)} %bitcast.202), channel_id=1, replica_groups=mesh['ctx'=16,'tp'=2] {'ctx'}, dimensions={0}, use_global_device_ids=true | all-gather | bytes 34816 | tf_op jit(solution)/shard_map/all_gather | solution.py:109
  180.0 18.7 %all-gather.7.cloned.1.call-done = bf16[1024,1024]{1,0:T(8,128)(2,1)} async-done(((bf16[64,1024]{1,0:T(8,128)(2,1)}), bf16[1024,1024]{1,0:T(8,128)(2,1)}) %all-gather.7.cloned.1.call-update) | async-done | bytes 2097168 | tf_op jit(solution)/shard_map/all_gather | solution.py:84
  198.6 3.8 %multiply_reduce_fusion = (f32[64,8]{0,1:T(8,128)S(1)}, bf16[8,128,64]{1,2,0:T(8,128)(2,1)}) fusion(f32[8,64,1024]{2,1,0:T(8,128)} %copy-done.2, f32[8,64]{1,0:T(8,128)S(1)} %log_add_fusion, pred[64,1024]{1,0:T(8,128)(4,1)S(1)} %broadcast_compare_fusion.1, bf16[1024,1024]{1,0:T(8,128)(2,1)} %all-gather.7.cloned.1.call-done, bf16[64,1024]{1,0:T(8,128)(2,1)S(1)} %copy-done.6), kind=kOutput, calls=%fused_computation.75 | convolution fusion | flops 136642048 | bytes 4526080 | tf_op jit(solution)/shard_map/hqk,khd->qhd/dot_general | solution.py:96
  202.4 38.9 %all-gather.1 = f32[16,64,8]{1,2,0:T(8,128)S(1)} all-gather(f32[1,64,8]{1,2,0:T(8,128)S(1)} %bitcast.203), channel_id=1, replica_groups=mesh['ctx'=16,'tp'=2] {'ctx'}, dimensions={0}, use_global_device_ids=true | all-gather | bytes 34816 | tf_op jit(solution)/shard_map/all_gather | solution.py:110
  241.4 19.7 %all-gather.11.cloned.1.call-done = bf16[1024,1024]{1,0:T(8,128)(2,1)} async-done(((bf16[64,1024]{1,0:T(8,128)(2,1)}), bf16[1024,1024]{1,0:T(8,128)(2,1)}) %all-gather.11.cloned.1.call-update) | async-done | bytes 2097168 | tf_op jit(solution)/shard_map/all_gather | solution.py:114
  261.1 2.7 select_exponential_fusion
  265.2 3.3 %fusion.75 = bf16[8,8,8,128]{3,2,1,0:T(8,128)(2,1)S(1)} fusion(f32[8,1024,64]{1,2,0:T(8,128)} %copy-done.1, bf16[1024,8,128]{0,2,1:T(8,128)(2,1)S(1)} %bitcast.199, f32[8,1024]{1,0:T(8,128)S(1)} %bitcast.200, bf16[1024,1024]{1,0:T(8,128)(2,1)} %all-gather.11.cloned.1.call-done, bf16[64,1024]{1,0:T(8,128)(2,1)S(1)} %copy-done.4), kind=kOutput, calls=%fused_computation.60 | convolution fusion | flops 270139392 | bytes 6586368 | tf_op jit(solution)/shard_map/hqk,qhd->khd/dot_general | solution.py:133
  268.6 2.5 fusion.14
  271.1 4.0 %fusion.79 = bf16[8,8,8,128]{3,2,1,0:T(8,128)(2,1)S(1)} fusion(f32[8,64,1024]{2,1,0:T(8,128)S(1)} %copy-done.3, f32[8,64]{1,0:T(8,128)S(1)} %bitcast.204, f32[8,64]{1,0:T(8,128)S(1)} %log_add_fusion, pred[64,1024]{1,0:T(8,128)(4,1)S(1)} %broadcast_compare_fusion.1, bf16[1024,1024]{1,0:T(8,128)(2,1)} %all-gather.7.cloned.1.call-done, ...), kind=kOutput, calls=%fused_computation.62 | convolution fusion | flops 271712256 | bytes 6623232 | tf_op jit(solution)/shard_map/hqk,khd->qhd/dot_general | solution.py:105
  275.1 2.4 fusion.47
  277.5 3.1 %fusion.44 = f32[64,1024]{1,0:T(8,128)} fusion(f32[64,1024]{1,0:T(8,128)S(1)} %fusion.47, bf16[3,1024,1024]{2,1,0:T(8,128)(2,1)} %param.10, bf16[8,8,8,128]{3,2,1,0:T(8,128)(2,1)S(1)} %fusion.78), kind=kOutput, calls=%fused_computation.47 | convolution fusion | flops 134283264 | bytes 2752512 | tf_op jit(solution)/shard_map/dot_general | solution.py:144
  285.9 1.4 reduce-scatter.2.cloned.1.call-done
  288.2 3.6 %collective-permute-start.2 = (bf16[64,512]{1,0:T(8,128)(2,1)S(1)}, bf16[64,512]{1,0:T(8,128)(2,1)S(1)}, u32[]{:S(2)}, u32[]{:S(2)}) collective-permute-start(bf16[64,512]{1,0:T(8,128)(2,1)S(1)} %convert_element_type.89), channel_id=1, source_target_pairs={{0,2},{2,4},{4,6},{6,8},{8,10},{10,12},{12,14},{14,16},{16,18},{18... | collective-permute-start | bytes 196616 | tf_op jit(solution)/shard_map/ppermute | solution.py:16
  293.8 4.2 %collective-permute-done.3 = bf16[64,512]{1,0:T(8,128)(2,1)S(1)} collective-permute-done((bf16[64,512]{1,0:T(8,128)(2,1)S(1)}, bf16[64,512]{1,0:T(8,128)(2,1)S(1)}, u32[]{:S(2)}, u32[]{:S(2)}) %collective-permute-start.3) | collective-permute-done | bytes 65568 | tf_op jit(solution)/shard_map/ppermute | solution.py:17
  (89 shorter events, 21.5 us)
Async XLA Ops:
  7.2 1.6 copy-start
  7.2 66.7 %all-gather.13.cloned.1.call-start = ((), (), s32[]{:S(2)}) async-start(), calls=%async_computation.4 | async-start | bytes 2228224 | tf_op jit(solution)/shard_map/all_gather | solution.py:115
  7.9 128.5 %all-gather.9.cloned.1.call-start = ((), (), s32[]{:S(2)}) async-start(), calls=%async_computation.2 | async-start | bytes 2228224 | tf_op jit(solution)/shard_map/all_gather | solution.py:83
  9.7 14.2 %collective-permute-start = (bf16[128,512]{1,0:T(8,128)(2,1)S(1)}, bf16[128,512]{1,0:T(8,128)(2,1)S(1)}, u32[]{:S(2)}, u32[]{:S(2)}) collective-permute-start(bf16[128,512]{1,0:T(8,128)(2,1)S(1)} %fusion.56), channel_id=1, source_target_pairs={{0,2},{2,4},{4,6},{6,8},{8,10},{10,12},{12,14},{14,16},{16,18},{18... | collective-permute-start | bytes 393224 | tf_op jit(solution)/shard_map/ppermute | solution.py:16
  14.5 9.3 %collective-permute-start.1 = (bf16[128,512]{1,0:T(8,128)(2,1)S(1)}, bf16[128,512]{1,0:T(8,128)(2,1)S(1)}, u32[]{:S(2)}, u32[]{:S(2)}) collective-permute-start(bf16[128,512]{1,0:T(8,128)(2,1)S(1)} %fusion.56), channel_id=1, source_target_pairs={{2,0},{4,2},{6,4},{8,6},{10,8},{12,10},{14,12},{16,14},{18,16},{20... | collective-permute-start | bytes 393224 | tf_op jit(solution)/shard_map/ppermute | solution.py:17
  28.8 169.9 %all-gather.7.cloned.1.call-start = ((), (), s32[]{:S(2)}) async-start(), calls=%async_computation.1 | async-start | bytes 2228224 | tf_op jit(solution)/shard_map/all_gather | solution.py:84
  31.5 3.7 %copy-start.9 = (s32[16]{0:T(128)S(1)}, s32[16]{0:T(128)}, u32[]{:S(2)}) copy-start(s32[16]{0:T(128)} %param.8) | copy-start | bytes 196
  31.5 229.6 %all-gather.11.cloned.1.call-start = ((), (), s32[]{:S(2)}) async-start(), calls=%async_computation.3 | async-start | bytes 2228224 | tf_op jit(solution)/shard_map/all_gather | solution.py:114
  34.4 252.9 %reduce-scatter.2.cloned.1.call-start = ((), (), s32[]{:S(2)}) async-start(), calls=%async_computation.5 | async-start | bytes 393216 | tf_op jit(solution)/shard_map/reduce_scatter | solution.py:147
  35.7 100.7 %copy-start.5 = (bf16[64,1024]{1,0:T(8,128)(2,1)S(1)}, bf16[64,1024]{1,0:T(8,128)(2,1)}, u32[]{:S(2)}) copy-start(bf16[64,1024]{1,0:T(8,128)(2,1)} %fusion.63) | copy-start | bytes 393220
  139.0 1.4 copy-start.2
  139.0 59.6 %copy-start.6 = (bf16[64,1024]{1,0:T(8,128)(2,1)S(1)}, bf16[64,1024]{1,0:T(8,128)(2,1)}, u32[]{:S(2)}) copy-start(bf16[64,1024]{1,0:T(8,128)(2,1)} %param.11) | copy-start | bytes 393220
  180.0 81.2 %copy-start.7 = (bf16[64,1024]{1,0:T(8,128)(2,1)S(1)}, bf16[64,1024]{1,0:T(8,128)(2,1)}, u32[]{:S(2)}) copy-start(bf16[64,1024]{1,0:T(8,128)(2,1)} %fusion.66) | copy-start | bytes 393220
  263.8 1.4 copy-start.1
  263.8 1.4 copy-start.4
  268.6 2.5 copy-start.3
  277.5 7.6 %copy-start.10 = (s32[256]{0:T(256)S(1)}, s32[256]{0:T(256)}, u32[]{:S(2)}) copy-start(s32[256]{0:T(256)} %param.7) | copy-start | bytes 3076
  277.5 15.6 %copy-start.8 = (bf16[8,128,64]{1,2,0:T(8,128)(2,1)S(1)}, bf16[8,128,64]{1,2,0:T(8,128)(2,1)}, u32[]{:S(2)}) copy-start(bf16[8,128,64]{1,2,0:T(8,128)(2,1)} %get-tuple-element.18) | copy-start | bytes 393220
  288.2 5.6 %collective-permute-start.2 = (bf16[64,512]{1,0:T(8,128)(2,1)S(1)}, bf16[64,512]{1,0:T(8,128)(2,1)S(1)}, u32[]{:S(2)}, u32[]{:S(2)}) collective-permute-start(bf16[64,512]{1,0:T(8,128)(2,1)S(1)} %convert_element_type.89), channel_id=1, source_target_pairs={{0,2},{2,4},{4,6},{6,8},{8,10},{10,12},{12,14},{14,16},{16,18},{18... | collective-permute-start | bytes 196616 | tf_op jit(solution)/shard_map/ppermute | solution.py:16
  291.8 6.2 %collective-permute-start.3 = (bf16[64,512]{1,0:T(8,128)(2,1)S(1)}, bf16[64,512]{1,0:T(8,128)(2,1)S(1)}, u32[]{:S(2)}, u32[]{:S(2)}) collective-permute-start(bf16[64,512]{1,0:T(8,128)(2,1)S(1)} %convert_element_type.89), channel_id=1, source_target_pairs={{2,0},{4,2},{6,4},{8,6},{10,8},{12,10},{14,12},{16,14},{18,16},{20... | collective-permute-start | bytes 196616 | tf_op jit(solution)/shard_map/ppermute | solution.py:17
Sparse Core Ops, SparseCore 0:
  10.8 63.0 all-gather.12
  77.2 59.1 all-gather.8
  139.2 59.3 all-gather.6
  201.8 59.2 all-gather.10
  280.7 6.5 reduce-scatter.1
where the time goes:
time: 306 us; the launch traced here: 305 us
  waiting for transfers between devices  143 us (47%)
  blocking collectives  79.7 us (26%)
  matrix products  35.5 us (12%)
  between operations  16.6 us (5%)
  local copies, waits for them, and re-layouts  13.3 us (4%)
  starting transfers between devices  11.3 us (4%)
  other arithmetic  6.49 us (2%)
    all_gather x1, waiting for transfers between devices, shards(): lax.all_gather(keyed, 'ctx', axis=0, tiled=True)  59.7 us
    all_gather x1, blocking collectives, shards(): lax.all_gather(delta, 'ctx', axis=0, tiled=True)  38.9 us
    all_gather x1, blocking collectives, shards(): lax.all_gather(lse_rows, 'ctx', axis=0, tiled=True)  38.9 us
    all_gather x1, waiting for transfers between devices, shards(): g_piece = lax.all_gather(d_attn, 'ctx', axis=0, tiled=True)  38.1 us
    all_gather x1, waiting for transfers between devices, shards(): q_piece = lax.all_gather(query, 'ctx', axis=0, tiled=True)  19.7 us
    all_gather x1, waiting for transfers between devices, shards(): lax.all_gather(valued, 'ctx', axis=0, tiled=True)  18.7 us
    ppermute x2, starting transfers between devices, extended_2(): before = lax.ppermute(last, axis, up)  8.48 us
  transfers between devices with their start and end apart: 9, of which 6 were waited for; matrix products, arithmetic and copies ran while one was open for 11% of the time, Pallas kernels for 0%

commit v1 on v0

v1 whole, which is shorter than its diff:
```python
import functools

import jax
import jax.numpy as jnp
from jax import lax
from jax.experimental import pallas as pl
from jax.experimental.pallas import tpu as pltpu
from jax.sharding import PartitionSpec as P

HD = 128
MESH = pl.DeviceIdType.MESH
VM = pl.BlockSpec(memory_space=pltpu.VMEM)


def remote(src, dst, send, recv, device):
    return pltpu.make_async_remote_copy(
        src_ref=src, dst_ref=dst, send_sem=send, recv_sem=recv, device_id=device, device_id_type=MESH
    )


def neighbours_kernel(n, blk_ref, out_ref, send_sem, recv_sem):
    me = lax.axis_index("ctx")
    left, right = lax.rem(me + n - 1, n), lax.rem(me + 1, n)
    barrier = pltpu.get_barrier_semaphore()
    for peer in (left, right):
        pl.semaphore_signal(barrier, inc=1, device_id={"ctx": peer}, device_id_type=MESH)
    pl.semaphore_wait(barrier, 2)
    copies = [
        remote(blk_ref.at[i], out_ref.at[i], send_sem.at[i], recv_sem.at[i], {"ctx": peer})
        for i, peer in enumerate((left, right))
    ]
    for copy in copies:
        copy.start()
    for copy in copies:
        copy.wait()


def neighbours(blk, n):
    return pl.pallas_call(
        functools.partial(neighbours_kernel, n),
        out_shape=jax.ShapeDtypeStruct(blk.shape, blk.dtype),
        in_specs=[VM],
        out_specs=VM,
        scratch_shapes=[pltpu.SemaphoreType.DMA((2,)), pltpu.SemaphoreType.DMA((2,))],
        compiler_params=pltpu.CompilerParams(collective_id=0, has_side_effects=True),
        name="neighbours",
    )(blk)


def attend_kernel(
    n, heads, rows, block,
    q_ref, k_ref, v_ref, g_ref, qid_ref, kid_ref,
    o_out, dq_out, dk_out, dv_out,
    qb, gb, kb, vb, ob, dqb, dkb, dvb, dka, dva,
    send_kv, recv_kv, send_qg, recv_qg, send_dkv, recv_dkv, send_odq, recv_odq, local_sem,
):
    groups = n // heads
    total = n * rows
    scale = HD ** (-0.5)
    me = lax.axis_index("ctx")
    my_head, my_group = me // groups, lax.rem(me, groups)

    def cols(head):
        return pl.ds(pl.multiple_of(head * HD, HD), HD)

    barrier = pltpu.get_barrier_semaphore()

    def greet(i, carry):
        peer = lax.rem(me + i, n)
        pl.semaphore_signal(barrier, inc=1, device_id={"ctx": peer}, device_id_type=MESH)
        return carry

    lax.fori_loop(1, n, greet, 0)
    pl.semaphore_wait(barrier, n - 1)

    def mate(i):
        return lax.rem(my_head + i, heads)

    def to_peer(i):
        peer = lax.rem(me + i, n)
        c = cols(peer // groups)
        return (
            remote(k_ref.at[:, c], kb.at[me], send_kv.at[0, i], recv_kv.at[0, i], {"ctx": peer}),
            remote(v_ref.at[:, c], vb.at[me], send_kv.at[1, i], recv_kv.at[1, i], {"ctx": peer}),
        )

    def to_mate(i):
        head = mate(i)
        peer = head * groups + my_group
        c = cols(head)
        return (
            remote(g_ref.at[:, c], gb.at[my_head], send_qg.at[0, i], recv_qg.at[0, i], {"ctx": peer}),
            remote(q_ref.at[:, c], qb.at[my_head], send_qg.at[1, i], recv_qg.at[1, i], {"ctx": peer}),
        )

    def back_peer(i):
        peer = lax.rem(me + i, n)
        c = cols(my_head)
        return (
            remote(dkb.at[peer], dk_out.at[my_group, :, c], send_dkv.at[0, i], recv_dkv.at[0, i], {"ctx": peer}),
            remote(dvb.at[peer], dv_out.at[my_group, :, c], send_dkv.at[1, i], recv_dkv.at[1, i], {"ctx": peer}),
        )

    def back_mate(i):
        head = mate(i)
        peer = head * groups + my_group
        c = cols(my_head)
        return (
            remote(ob.at[head], o_out.at[:, c], send_odq.at[0, i], recv_odq.at[0, i], {"ctx": peer}),
            remote(dqb.at[head], dq_out.at[:, c], send_odq.at[1, i], recv_odq.at[1, i], {"ctx": peer}),
        )

    def start_all(make):
        def body(i, carry):
            for copy in make(i):
                copy.start()
            return carry
        return body

    def wait_all(make):
        def body(i, carry):
            for copy in make(i):
                copy.wait()
            return carry
        return body

    lax.fori_loop(1, n, start_all(to_peer), 0)
    lax.fori_loop(1, heads, start_all(to_mate), 0)
    mine = cols(my_head)
    own = [
        pltpu.make_async_copy(src.at[:, mine], dst, local_sem.at[i])
        for i, (src, dst) in enumerate((
            (k_ref, kb.at[me]), (v_ref, vb.at[me]), (g_ref, gb.at[my_head]), (q_ref, qb.at[my_head])
        ))
    ]
    for copy in own:
        copy.start()
    dka[...] = jnp.zeros_like(dka)
    dva[...] = jnp.zeros_like(dva)
    for copy in own:
        copy.wait()
    lax.fori_loop(1, heads, wait_all(to_mate), 0)
    lax.fori_loop(1, n, wait_all(to_peer), 0)

    over_last = (((1,), (1,)), ((), ()))
    over_first = (((0,), (0,)), ((), ()))

    def step(b, carry):
        first = b * block
        q = qb[pl.ds(first, block)].reshape(block * rows, HD)
        g = gb[pl.ds(first, block)].reshape(block * rows, HD)
        k = kb[...].reshape(total, HD)
        v = vb[...].reshape(total, HD)
        qid = qid_ref[pl.ds(pl.multiple_of(first * rows, rows), block * rows), :]
        allowed = qid >= kid_ref[...]
        score = lax.dot_general(q, k, over_last, preferred_element_type=jnp.float32) * scale
        score = jnp.where(allowed, score, -jnp.inf)
        top = jnp.max(score, axis=1, keepdims=True)
        e = jnp.exp(score - top)
        prob = e * (1.0 / jnp.sum(e, axis=1, keepdims=True))
        probs = prob.astype(jnp.bfloat16)
        out = jnp.dot(probs, v, preferred_element_type=jnp.float32).astype(jnp.bfloat16)
        delta = jnp.sum(g.astype(jnp.float32) * out.astype(jnp.float32), axis=1, keepdims=True)
        dprob = lax.dot_general(g, v, over_last, preferred_element_type=jnp.float32)
        dscore = (prob * (dprob - delta)).astype(jnp.bfloat16)
        dq = (jnp.dot(dscore, k, preferred_element_type=jnp.float32) * scale).astype(jnp.bfloat16)
        ob[pl.ds(first, block)] = out.reshape(block, rows, HD)
        dqb[pl.ds(first, block)] = dq.reshape(block, rows, HD)
        dka[...] += lax.dot_general(dscore, q, over_first, preferred_element_type=jnp.float32)
        dva[...] += lax.dot_general(probs, g, over_first, preferred_element_type=jnp.float32)
        return carry

    lax.fori_loop(0, heads // block, step, 0)
    dkb[...] = (dka[...] * scale).astype(jnp.bfloat16).reshape(n, rows, HD)
    dvb[...] = dva[...].astype(jnp.bfloat16).reshape(n, rows, HD)

    lax.fori_loop(1, n, start_all(back_peer), 0)
    lax.fori_loop(1, heads, start_all(back_mate), 0)
    own = [
        pltpu.make_async_copy(src, dst, local_sem.at[i])
        for i, (src, dst) in enumerate((
            (dkb.at[me], dk_out.at[my_group, :, mine]), (dvb.at[me], dv_out.at[my_group, :, mine]),
            (ob.at[my_head], o_out.at[:, mine]), (dqb.at[my_head], dq_out.at[:, mine]),
        ))
    ]
    for copy in own:
        copy.start()
    for copy in own:
        copy.wait()
    lax.fori_loop(1, heads, wait_all(back_mate), 0)
    lax.fori_loop(1, n, wait_all(back_peer), 0)


def attend(query, keyed, valued, grad, qid, kid, n):
    rows, feats = query.shape
    heads = feats // HD
    groups = n // heads
    total = n * rows
    block = 2 if heads % 2 == 0 else 1
    bf = jnp.bfloat16
    dma = pltpu.SemaphoreType.DMA
    return pl.pallas_call(
        functools.partial(attend_kernel, n, heads, rows, block),
        out_shape=[
            jax.ShapeDtypeStruct((rows, feats), bf),
            jax.ShapeDtypeStruct((rows, feats), bf),
            jax.ShapeDtypeStruct((groups, rows, feats), bf),
            jax.ShapeDtypeStruct((groups, rows, feats), bf),
        ],
        in_specs=[VM] * 6,
        out_specs=[VM] * 4,
        scratch_shapes=[
            pltpu.VMEM((heads, rows, HD), bf), pltpu.VMEM((heads, rows, HD), bf),
            pltpu.VMEM((n, rows, HD), bf), pltpu.VMEM((n, rows, HD), bf),
            pltpu.VMEM((heads, rows, HD), bf), pltpu.VMEM((heads, rows, HD), bf),
            pltpu.VMEM((n, rows, HD), bf), pltpu.VMEM((n, rows, HD), bf),
            pltpu.VMEM((total, HD), jnp.float32), pltpu.VMEM((total, HD), jnp.float32),
            dma((2, n)), dma((2, n)), dma((2, heads)), dma((2, heads)),
            dma((2, n)), dma((2, n)), dma((2, heads)), dma((2, heads)), dma((4,)),
        ],
        compiler_params=pltpu.CompilerParams(
            collective_id=1, has_side_effects=True, vmem_limit_bytes=48 << 20
        ),
        name="attend",
    )(query, keyed, valued, grad, qid, kid)


def returning_kernel(n, tp, half, rows, part_ref, own_ref, lo_ref, hi_ref, send_sem, recv_sem, local_sem):
    me, mt = lax.axis_index("ctx"), lax.axis_index("tp")
    left, right = lax.rem(me + n - 1, n), lax.rem(me + 1, n)
    peers = [(me, lax.rem(mt + i, tp)) for i in range(1, tp)]
    peers += [(side, lax.rem(mt + i, tp)) for side in (left, right) for i in range(tp)]
    barrier = pltpu.get_barrier_semaphore()
    for peer in peers:
        pl.semaphore_signal(barrier, inc=1, device_id=peer, device_id_type=MESH)
    pl.semaphore_wait(barrier, len(peers))
    first, last = pl.ds(0, half), pl.ds(rows - half, half)
    copies = []
    for at, (c, t) in enumerate(peers):
        if at < tp - 1:
            src, dst = part_ref.at[t], own_ref.at[mt]
        elif at < 2 * tp - 1:
            src, dst = part_ref.at[t, first], hi_ref.at[mt]
        else:
            src, dst = part_ref.at[t, last], lo_ref.at[mt]
        copies.append(remote(src, dst, send_sem.at[at], recv_sem.at[at], (c, t)))
    for copy in copies:
        copy.start()
    mine = pltpu.make_async_copy(part_ref.at[mt], own_ref.at[mt], local_sem)
    mine.start()
    mine.wait()
    for copy in copies:
        copy.wait()


def returning(part, n):
    tp, rows, width = part.shape
    half = rows // 2
    dma = pltpu.SemaphoreType.DMA
    return pl.pallas_call(
        functools.partial(returning_kernel, n, tp, half, rows),
        out_shape=[
            jax.ShapeDtypeStruct((tp, rows, width), part.dtype),
            jax.ShapeDtypeStruct((tp, half, width), part.dtype),
            jax.ShapeDtypeStruct((tp, half, width), part.dtype),
        ],
        in_specs=[VM],
        out_specs=[VM] * 3,
        scratch_shapes=[dma((3 * tp - 1,)), dma((3 * tp - 1,)), dma],
        compiler_params=pltpu.CompilerParams(collective_id=2, has_side_effects=True),
        name="returning",
    )(part)


def shards(byte_states, patch_of_byte, patch_first, moved, w_qkv, d_attn):
    me = lax.axis_index("ctx")
    n = lax.axis_size("ctx")
    tp = lax.axis_size("tp")
    rows, feats = d_attn.shape
    half = rows // 2
    heads = feats // HD
    groups = n // heads
    total = rows * n
    model = byte_states.shape[1]
    zero_one = jnp.zeros((1,), jnp.int32)
    ends = jnp.concatenate([patch_first[1:], jnp.full((1,), total, jnp.int32)])
    counts = ends - patch_first
    lower, upper = moved[0], moved[1]
    below = jnp.concatenate([zero_one, upper[:-1]])
    above = jnp.concatenate([lower[1:], zero_one])
    ranks = jnp.arange(rows, dtype=jnp.int32)[None, :]
    ids = jnp.where(
        ranks < below[:, None],
        patch_first[:, None] - below[:, None] + ranks,
        jnp.where(
            ranks >= (rows - above)[:, None],
            ends[:, None] + ranks - (rows - above)[:, None],
            patch_first[:, None] + lower[:, None] + ranks - below[:, None],
        ),
    )
    kid = ids.reshape(1, total)
    qid = lax.dynamic_index_in_dim(
        ids.reshape(heads, groups, rows), lax.rem(me, groups), 1, keepdims=False
    ).reshape(heads * rows, 1)

    def own(values):
        return lax.dynamic_index_in_dim(values, me, 0, keepdims=False)

    my_count, my_low, my_high = own(counts), own(lower), own(upper)
    my_below, my_above = own(below), own(above)
    rank = jnp.arange(rows, dtype=jnp.int32)
    part_rank = jnp.arange(half, dtype=jnp.int32)
    own_local = jnp.where(
        (rank >= my_below) & (rank < rows - my_above), my_low + rank - my_below, -1
    )
    down = part_rank - half + my_low
    up = jnp.where(part_rank < my_high, my_count - my_high + part_rank, -1)
    wanted = jnp.concatenate([down, up, own_local])
    member = patch_of_byte[None, :] == wanted[:, None]
    lengths = jnp.sum(member.astype(jnp.float32), axis=1)
    pooled_all = (
        jnp.dot(member.astype(jnp.bfloat16), byte_states, preferred_element_type=jnp.float32)
        / jnp.maximum(lengths, 1.0)[:, None]
    ).astype(jnp.bfloat16)
    came = neighbours(pooled_all[: 2 * half].reshape(2, half, model), n)
    pooled = pooled_all[2 * half :] + jnp.concatenate([came[1], came[0]], axis=0)
    query = jnp.dot(pooled, w_qkv[0], preferred_element_type=jnp.float32).astype(jnp.bfloat16)
    keyed = jnp.dot(pooled, w_qkv[1], preferred_element_type=jnp.float32).astype(jnp.bfloat16)
    valued = jnp.dot(pooled, w_qkv[2], preferred_element_type=jnp.float32).astype(jnp.bfloat16)
    attn_out, d_query, d_key, d_value = attend(query, keyed, valued, d_attn, qid, kid, n)
    d_key = jnp.sum(d_key.astype(jnp.float32), axis=0).astype(jnp.bfloat16)
    d_value = jnp.sum(d_value.astype(jnp.float32), axis=0).astype(jnp.bfloat16)
    contract = (((1,), (1,)), ((), ()))
    partial = lax.dot_general(d_query, w_qkv[0], contract, preferred_element_type=jnp.float32)
    partial += lax.dot_general(d_key, w_qkv[1], contract, preferred_element_type=jnp.float32)
    partial += lax.dot_general(d_value, w_qkv[2], contract, preferred_element_type=jnp.float32)
    width = model // tp
    part = jnp.transpose(partial.astype(jnp.bfloat16).reshape(rows, tp, width), (1, 0, 2))
    own_part, lo_part, hi_part = returning(part, n)
    stacked = jnp.concatenate([lo_part, own_part, hi_part], axis=1)
    returned = jnp.sum(stacked.astype(jnp.float32), axis=0).astype(jnp.bfloat16)
    target = jnp.where(
        patch_of_byte < my_low,
        half - my_low + patch_of_byte,
        jnp.where(
            patch_of_byte >= my_count - my_high,
            half + rows + patch_of_byte - (my_count - my_high),
            half + my_below + patch_of_byte - my_low,
        ),
    )
    chooser = (target[:, None] == jnp.arange(2 * rows, dtype=jnp.int32)[None, :]).astype(jnp.bfloat16)
    spread = jnp.dot(chooser, returned, preferred_element_type=jnp.float32)
    same = (patch_of_byte[:, None] == patch_of_byte[None, :]).astype(jnp.float32)
    byte_lengths = jnp.sum(same, axis=1)
    byte_grad = (spread / byte_lengths[:, None]).astype(jnp.bfloat16)
    return attn_out, byte_grad


def solution(mesh):
    placed = (P("ctx", None), P("ctx"), P(), P(), P(None, None, "tp"), P("ctx", "tp"))
    return jax.shard_map(
        shards,
        mesh=mesh,
        in_specs=placed,
        out_specs=(P("ctx", "tp"), P("ctx", "tp")),
        check_vma=False,
    )
```

time: 306 us -> 102 us (0.33)
  waiting for transfers between devices: 143 us -> 0 us
  blocking collectives: 79.7 us -> 0 us
  Pallas kernels: 0 us -> 66.1 us
  matrix products: 35.5 us -> 15.2 us
  between operations: 16.6 us -> 4.15 us
  starting transfers between devices: 11.3 us -> 0 us
  local copies, waits for them, and re-layouts: 13.3 us -> 9.66 us
    all_gather x4 -> x0, waiting for transfers between devices: 136 us -> none  [the longest x1 59.7 us: shards(): lax.all_gather(keyed, 'ctx', axis=0, tiled=True)]
    all_gather x3 -> x0, blocking collectives: 79.7 us -> none  [the longest x1 38.9 us: shards(): lax.all_gather(delta, 'ctx', axis=0, tiled=True)]
    pallas_call x0 -> x3, Pallas kernels: none -> 66.1 us  [the longest x1 44.5 us: attend(): pl.pallas_call(functools.partial(attend_kernel, n, heads, rows, block), o...]
    dot_general x9 -> x2, matrix products: 19.4 us -> 1.95 us  [the longest x1 0.99 us: shards(): spread = jnp.dot(chooser, returned, preferred_element_type=jnp.float32)]
    ppermute x4 -> x0, starting transfers between devices: 11.1 us -> none  [the longest x2 8.48 us: extended_2(): before = lax.ppermute(last, axis, up)]
    ppermute x4 -> x0, waiting for transfers between devices: 4.18 us -> none  [the longest x2 4.17 us: extended_2(): after = lax.ppermute(first, axis, down)]
  transfers between devices with their start and end apart: 9 -> 0, of which waited for: 6 -> 0; matrix products, arithmetic and copies ran while one was open for 11% -> 0% of each run, Pallas kernels for 0% -> 0%
where the time goes in v1:
time: 102 us
  Pallas kernels  66.1 us (65%)
  matrix products  15.2 us (15%)
  local copies, waits for them, and re-layouts  9.66 us (9%)
  other arithmetic  6.46 us (6%)
  between operations  4.15 us (4%)
    pallas_call x1, Pallas kernels, attend(): pl.pallas_call(functools.partial(attend_kernel, n, heads, rows, block), o...  44.5 us
    pallas_call x1, Pallas kernels, neighbours(): pl.pallas_call(functools.partial(neighbours_kernel, n), out_shape=jax.Sha...  11.3 us
    pallas_call x1, Pallas kernels, returning(): pl.pallas_call(functools.partial(returning_kernel, n, tp, half, rows), ou...  10.4 us
    dynamic_slice x4, local copies, waits for them, and re-layouts, own(): return lax.dynamic_index_in_dim(values, me, 0, keepdims=False)  2.57 us
    dot_general x1, matrix products, shards(): lax.dot_general(d_query, w_qkv[0], contract, preferred_element_type=jnp.f...  2.36 us
    dot_general x1, matrix products, shards(): lax.dot_general(d_key, w_qkv[1], contract, preferred_element_type=jnp.flo...  2.35 us
    dot_general x1, matrix products, shards(): lax.dot_general(d_value, w_qkv[2], contract, preferred_element_type=jnp.f...  2.35 us
    dot_general x1, matrix products, shards(): jnp.dot(pooled, w_qkv[0], preferred_element_type=jnp.float32)  2.08 us

profile of v1, /device:TPU:0, one launch (start us, length us, event | category | flops | bytes accessed | tf_op | source)
XLA Modules:
  0.0 101.6 jit_solution(9191888879632919723)
XLA Ops:
  0.7 0.8 slice_bitcast_fusion.3
  1.5 0.7 slice.49
  2.2 0.8 pad_add_fusion
  3.6 0.8 fusion.50
  5.1 0.7 dynamic_slice.24
  6.4 1.3 %and_select_fusion = s32[64]{0:T(128)S(1)} fusion(s32[]{:T(128)} %bitcast, s32[]{:T(128)} %bitcast.6, s32[]{:T(128)} %bitcast.4), kind=kLoop, calls=%fused_computation.54 | loop fusion | flops 384 | bytes 268 | tf_op jit(solution)/shard_map/jit(_where)/select_n | solution.py:313
  7.7 0.7 dynamic_slice.22
  11.1 0.8 fusion.39
  12.0 1.0 fusion.19
  12.9 0.7 slice.62
  13.6 11.3 %neighbours.1 = bf16[2,32,1024]{2,1,0:T(8,128)(2,1)} custom-call(bf16[2,32,1024]{2,1,0:T(8,128)(2,1)} %bitcast.61), custom_call_target="tpu_custom_call" | custom-call | tf_op jit(solution)/shard_map/neighbours/pallas_call | solution.py:39
  24.9 0.9 slice_bitcast_fusion.1
  25.8 2.1 %fusion.35.v_ref = bf16[64,1024]{1,0:T(8,128)(2,1)S(1)} fusion(bf16[3,1024,1024]{2,1,0:T(8,128)(2,1)} %param.10, bf16[128,1024]{1,0:T(8,128)(2,1)S(1)} %fusion.19, bf16[32,1024]{1,0:T(8,128)(2,1)S(1)} %get-tuple-element.17, bf16[32,1024]{1,0:T(8,128)(2,1)S(1)} %get-tuple-element.16), kind=kOutput, calls=%fused_computation.27 | convolution fusion | flops 134676480 | bytes 2490368 | tf_op jit(solution)/shard_map/dot_general | solution.py:329
  27.9 2.1 %fusion.32.k_ref = bf16[64,1024]{1,0:T(8,128)(2,1)S(1)} fusion(bf16[3,1024,1024]{2,1,0:T(8,128)(2,1)} %param.10, bf16[128,1024]{1,0:T(8,128)(2,1)S(1)} %fusion.19, bf16[32,1024]{1,0:T(8,128)(2,1)S(1)} %get-tuple-element.17, bf16[32,1024]{1,0:T(8,128)(2,1)S(1)} %get-tuple-element.16), kind=kOutput, calls=%fused_computation.26 | convolution fusion | flops 134676480 | bytes 2490368 | tf_op jit(solution)/shard_map/dot_general | solution.py:328
  30.0 2.1 %fusion.29.q_ref = bf16[64,1024]{1,0:T(8,128)(2,1)S(1)} fusion(bf16[3,1024,1024]{2,1,0:T(8,128)(2,1)} %param.10, bf16[128,1024]{1,0:T(8,128)(2,1)S(1)} %fusion.19, bf16[32,1024]{1,0:T(8,128)(2,1)S(1)} %get-tuple-element.17, bf16[32,1024]{1,0:T(8,128)(2,1)S(1)} %get-tuple-element.16), kind=kOutput, calls=%fused_computation.25 | convolution fusion | flops 134676480 | bytes 2490368 | tf_op jit(solution)/shard_map/dot_general | solution.py:327
  34.2 44.5 %attend.1 = (bf16[64,1024]{1,0:T(8,128)(2,1)S(1)}, bf16[64,1024]{1,0:T(8,128)(2,1)S(1)}, bf16[2,64,1024]{2,1,0:T(8,128)(2,1)S(1)}, bf16[2,64,1024]{2,1,0:T(8,128)(2,1)S(1)}) custom-call(bf16[64,1024]{1,0:T(8,128)(2,1)S(1)} %fusion.29.q_ref, bf16[64,1024]{1,0:T(8,128)(2,1)S(1)} %fusion.32.k_ref, bf16[64,1024]{1,0:T(8,128)(2,1)S(1)} %fusion.35.v_ref, ...), custom_call_target="tpu_custom_call" | custom-call | tf_op jit(solution)/shard_map/attend/pallas_call | solution.py:202
  78.7 2.4 %fusion = f32[64,1024]{1,0:T(8,128)S(1)} fusion(bf16[64,1024]{1,0:T(8,128)(2,1)S(1)} %reduce_sum.56, bf16[3,1024,1024]{2,1,0:T(8,128)(2,1)} %param.10), kind=kOutput, calls=%fused_computation | convolution fusion | flops 134217728 | bytes 2490368 | tf_op jit(solution)/shard_map/dot_general | solution.py:336
  81.1 2.4 %fusion.4 = f32[64,1024]{1,0:T(8,128)S(1)} fusion(bf16[64,1024]{1,0:T(8,128)(2,1)S(1)} %reduce_sum.55, bf16[3,1024,1024]{2,1,0:T(8,128)(2,1)} %param.10), kind=kOutput, calls=%fused_computation.4 | convolution fusion | flops 134217728 | bytes 2490368 | tf_op jit(solution)/shard_map/dot_general | solution.py:335
  83.5 2.4 %fusion.26 = bf16[64,1024]{1,0:T(8,128)(2,1)S(1)} fusion(f32[64,1024]{1,0:T(8,128)S(1)} %fusion, f32[64,1024]{1,0:T(8,128)S(1)} %fusion.4, bf16[64,1024]{1,0:T(8,128)(2,1)S(1)} %get-tuple-element.10, bf16[3,1024,1024]{2,1,0:T(8,128)(2,1)} %param.10), kind=kOutput, calls=%fused_computation.24 | convolution fusion | flops 134414336 | bytes 2883584 | tf_op jit(solution)/shard_map/dot_general | solution.py:334
  85.8 0.7 copy.29
  86.5 10.4 %returning.1 = (bf16[2,64,512]{2,1,0:T(8,128)(2,1)}, bf16[2,32,512]{2,1,0:T(8,128)(2,1)}, bf16[2,32,512]{2,1,0:T(8,128)(2,1)}) custom-call(bf16[2,64,512]{2,1,0:T(8,128)(2,1)} %bitcast.60), custom_call_target="tpu_custom_call" | custom-call | tf_op jit(solution)/shard_map/returning/pallas_call | solution.py:260
  96.9 1.0 maximum_reduce_fusion
  100.0 1.0 fusion.18
  101.0 0.7 copy.31
  (46 shorter events, 5.7 us)
Async XLA Ops:
  0.6 11.3 %copy-start = (bf16[256,1024]{1,0:T(8,128)(2,1)S(1)}, bf16[256,1024]{1,0:T(8,128)(2,1)}, u32[]{:S(2)}) copy-start(bf16[256,1024]{1,0:T(8,128)(2,1)} %param.6) | copy-start | bytes 1572868
  0.6 33.5 %copy-start.1 = (bf16[64,1024]{1,0:T(8,128)(2,1)S(1)}, bf16[64,1024]{1,0:T(8,128)(2,1)}, u32[]{:S(2)}) copy-start(bf16[64,1024]{1,0:T(8,128)(2,1)} %g_ref.1) | copy-start | bytes 393220
  30.0 69.2 %copy-start.2 = (s32[256]{0:T(256)S(1)}, s32[256]{0:T(256)}, u32[]{:S(2)}) copy-start(s32[256]{0:T(256)} %param.7) | copy-start | bytes 3076

commit v2 on v0

v2 whole, which is shorter than its diff:
```python
import functools

import jax
import jax.numpy as jnp
from jax import lax
from jax.experimental import pallas as pl
from jax.experimental.pallas import tpu as pltpu
from jax.sharding import PartitionSpec as P

HD = 128
MESH = pl.DeviceIdType.MESH
VM = pl.BlockSpec(memory_space=pltpu.VMEM)


def remote(src, dst, send, recv, device):
    return pltpu.make_async_remote_copy(
        src_ref=src, dst_ref=dst, send_sem=send, recv_sem=recv, device_id=device, device_id_type=MESH
    )


def whole_kernel(
    n, tp, heads, rows, block,
    bytes_ref, pob_ref, first_ref, moved_ref, w_ref, d_ref,
    attn_ref, grad_ref,
    blk, came, pooled, wbuf, own3, qb, gb, kb, vb, ob, dqb, dkb, dvb, dka, dva,
    o_in, dq_in, dk_in, dv_in, part, own_part, lo_part, hi_part,
    w_sem, send_nb, recv_nb, send_kv, recv_kv, send_qg, recv_qg,
    send_dkv, recv_dkv, send_odq, recv_odq, send_rt, recv_rt, local_sem,
):
    groups = n // heads
    total = n * rows
    half = rows // 2
    scale = HD ** (-0.5)
    bf, f32 = jnp.bfloat16, jnp.float32
    me, mt = lax.axis_index("ctx"), lax.axis_index("tp")
    my_head, my_group = me // groups, lax.rem(me, groups)
    left, right = lax.rem(me + n - 1, n), lax.rem(me + 1, n)
    width = part.shape[2]

    def cols(head):
        return pl.ds(pl.multiple_of(head * HD, HD), HD)

    barrier = pltpu.get_barrier_semaphore()

    def greet(i, carry):
        peer = lax.rem(me + i, n)
        pl.semaphore_signal(barrier, inc=1, device_id=(peer, mt), device_id_type=MESH)
        return carry

    lax.fori_loop(1, n, greet, 0)
    for c in (me, left, right):
        for i in range(1, tp):
            pl.semaphore_signal(
                barrier, inc=1, device_id=(c, lax.rem(mt + i, tp)), device_id_type=MESH
            )
    loads = [pltpu.make_async_copy(w_ref.at[j], wbuf.at[j], w_sem.at[j]) for j in range(3)]
    for j in (1, 2, 0):
        loads[j].start()

    def plan(c):
        below = moved_ref[1, lax.rem(c + n - 1, n)]
        above = moved_ref[0, lax.rem(c + 1, n)]
        start = first_ref[c]
        end = jnp.where(c == n - 1, total, first_ref[lax.rem(c + 1, n)])
        return start, end, below, above, moved_ref[0, c], moved_ref[1, c]

    def numbers(c, rank):
        start, end, below, above, low, high = plan(c)
        return jnp.where(
            rank < below,
            start - below + rank,
            jnp.where(rank >= rows - above, end + rank - (rows - above), start + low + rank - below),
        )

    start, end, below, above, low, high = plan(me)
    count = end - start
    rank = lax.broadcasted_iota(jnp.int32, (2 * rows, 1), 0)
    own_rank = rank - 2 * half
    own_local = jnp.where((own_rank >= below) & (own_rank < rows - above), low + own_rank - below, -1)
    up = jnp.where(rank - half < high, count - high + rank - half, -1)
    wanted = jnp.where(rank < half, rank - half + low, jnp.where(rank < 2 * half, up, own_local))
    pob = pob_ref[...]
    member = (pob == wanted).astype(f32)
    lengths = jnp.maximum(jnp.sum(member, axis=1, keepdims=True), 1.0)
    means = (
        jnp.dot(member.astype(bf), bytes_ref[...], preferred_element_type=f32) / lengths
    ).astype(bf)
    blk[0] = means[:half]
    blk[1] = means[half : 2 * half]
    pl.semaphore_wait(barrier, n - 1 + 3 * (tp - 1))
    near = [
        remote(blk.at[i], came.at[i], send_nb.at[i], recv_nb.at[i], (peer, mt))
        for i, peer in enumerate((left, right))
    ]
    for copy in near:
        copy.start()

    def over_peers(make, wait=False):
        def body(i, carry):
            copy = make(i)
            if wait:
                copy.wait()
            else:
                copy.start()
            return carry

        lax.fori_loop(1, n, body, 0)

    def over_mates(make, wait=False):
        def body(i, carry):
            copy = make(i)
            if wait:
                copy.wait()
            else:
                copy.start()
            return carry

        lax.fori_loop(1, heads, body, 0)

    def to_peer(a, ref, out):
        def make(i):
            peer = lax.rem(me + i, n)
            return remote(
                ref.at[:, cols(peer // groups)], out.at[me], send_kv.at[a, i], recv_kv.at[a, i], (peer, mt)
            )

        return make

    def to_mate(a, ref, out):
        def make(i):
            head = lax.rem(my_head + i, heads)
            return remote(
                ref.at[:, cols(head)], out.at[my_head], send_qg.at[a, i], recv_qg.at[a, i],
                (head * groups + my_group, mt),
            )

        return make

    def back_peer(a, ref, out):
        def make(i):
            peer = lax.rem(me + i, n)
            return remote(
                ref.at[peer], out.at[my_group, :, cols(my_head)], send_dkv.at[a, i], recv_dkv.at[a, i],
                (peer, mt),
            )

        return make

    def back_mate(a, ref, out):
        def make(i):
            head = lax.rem(my_head + i, heads)
            return remote(
                ref.at[head], out.at[:, cols(my_head)], send_odq.at[a, i], recv_odq.at[a, i],
                (head * groups + my_group, mt),
            )

        return make

    mine = cols(my_head)
    send_g = to_mate(0, d_ref, gb)
    send_q = to_mate(1, own3.at[0], qb)
    send_k = to_peer(0, own3.at[1], kb)
    send_v = to_peer(1, own3.at[2], vb)
    over_mates(send_g)
    for copy in near:
        copy.wait()
    pooled[pl.ds(0, half)] = means[2 * half : 3 * half] + came[1]
    pooled[pl.ds(half, half)] = means[3 * half :] + came[0]
    for j, send in ((1, lambda: over_peers(send_k)), (2, lambda: over_peers(send_v)), (0, lambda: over_mates(send_q))):
        loads[j].wait()
        own3[j] = jnp.dot(pooled[...], wbuf[j], preferred_element_type=f32).astype(bf)
        send()
    own = [
        pltpu.make_async_copy(src, dst, local_sem.at[i])
        for i, (src, dst) in enumerate((
            (own3.at[1, :, mine], kb.at[me]), (own3.at[2, :, mine], vb.at[me]),
            (d_ref.at[:, mine], gb.at[my_head]), (own3.at[0, :, mine], qb.at[my_head]),
        ))
    ]
    for copy in own:
        copy.start()
    dka[...] = jnp.zeros_like(dka)
    dva[...] = jnp.zeros_like(dva)
    lane = lax.broadcasted_iota(jnp.int32, (1, total), 1)

    def number_keys(c, ids):
        return jnp.where((lane >= c * rows) & (lane < (c + 1) * rows), numbers(c, lane - c * rows), ids)

    kid = lax.fori_loop(0, n, number_keys, jnp.zeros((1, total), jnp.int32))
    for copy in own:
        copy.wait()
    over_mates(send_g, True)
    over_peers(send_k, True)
    over_peers(send_v, True)
    over_mates(send_q, True)

    over_last = (((1,), (1,)), ((), ()))
    over_first = (((0,), (0,)), ((), ()))
    back_o, back_q = back_mate(0, ob, o_in), back_mate(1, dqb, dq_in)
    row = lax.broadcasted_iota(jnp.int32, (rows, 1), 0)
    step_keys = 128 // rows if rows < 128 else 1
    for b in range(heads // block):
        lo = b * block
        reach = min(n, (lo + block) * groups + 1)
        reach = min(n, -(-reach // step_keys) * step_keys)
        keys = reach * rows
        q = qb[pl.ds(lo, block)].reshape(block * rows, HD)
        g = gb[pl.ds(lo, block)].reshape(block * rows, HD)
        k = kb[pl.ds(0, reach)].reshape(keys, HD)
        v = vb[pl.ds(0, reach)].reshape(keys, HD)
        qid = jnp.concatenate([numbers((lo + j) * groups + my_group, row) for j in range(block)], axis=0)
        allowed = qid >= kid[:, :keys]
        score = lax.dot_general(q, k, over_last, preferred_element_type=f32) * scale
        score = jnp.where(allowed, score, -jnp.inf)
        top = jnp.max(score, axis=1, keepdims=True)
        e = jnp.exp(score - top)
        prob = e * (1.0 / jnp.sum(e, axis=1, keepdims=True))
        probs = prob.astype(bf)
        out = jnp.dot(probs, v, preferred_element_type=f32).astype(bf)
        delta = jnp.sum(g.astype(f32) * out.astype(f32), axis=1, keepdims=True)
        dprob = lax.dot_general(g, v, over_last, preferred_element_type=f32)
        dscore = (prob * (dprob - delta)).astype(bf)
        dq = (jnp.dot(dscore, k, preferred_element_type=f32) * scale).astype(bf)
        ob[pl.ds(lo, block)] = out.reshape(block, rows, HD)
        dqb[pl.ds(lo, block)] = dq.reshape(block, rows, HD)
        dka[pl.ds(0, keys)] += lax.dot_general(dscore, q, over_first, preferred_element_type=f32)
        dva[pl.ds(0, keys)] += lax.dot_general(probs, g, over_first, preferred_element_type=f32)
        for j in range(block):
            i = lax.rem(lo + j - my_head + heads, heads)

            @pl.when(i != 0)
            def _():
                back_o(i).start()
                back_q(i).start()

    send_dk, send_dv = back_peer(0, dkb, dk_in), back_peer(1, dvb, dv_in)
    dvb[...] = dva[...].astype(bf).reshape(n, rows, HD)
    over_peers(send_dv)
    dkb[...] = (dka[...] * scale).astype(bf).reshape(n, rows, HD)
    over_peers(send_dk)
    own = [
        pltpu.make_async_copy(src, dst, local_sem.at[i])
        for i, (src, dst) in enumerate((
            (dkb.at[me], dk_in.at[my_group, :, mine]), (dvb.at[me], dv_in.at[my_group, :, mine]),
            (ob.at[my_head], o_in.at[:, mine]), (dqb.at[my_head], dq_in.at[:, mine]),
        ))
    ]
    for copy in own:
        copy.start()
    for copy in own:
        copy.wait()
    over_mates(back_o, True)
    attn_ref[...] = o_in[...]
    over_mates(back_q, True)
    partial = lax.dot_general(dq_in[...], wbuf[0], over_last, preferred_element_type=f32)
    for send, held, j in ((send_dv, dv_in, 2), (send_dk, dk_in, 1)):
        over_peers(send, True)
        summed = held[0].astype(f32)
        for i in range(1, groups):
            summed = summed + held[i].astype(f32)
        partial += lax.dot_general(summed.astype(bf), wbuf[j], over_last, preferred_element_type=f32)
    for t in range(tp):
        part[t] = partial[:, t * width : (t + 1) * width].astype(bf)
    edge_lo, edge_hi = pl.ds(0, half), pl.ds(rows - half, half)
    copies = []
    for i in range(1, tp):
        t = lax.rem(mt + i, tp)
        copies.append((part.at[t], own_part.at[mt], (me, t)))
    for i in range(tp):
        t = lax.rem(mt + i, tp)
        copies.append((part.at[t, edge_lo], hi_part.at[mt], (left, t)))
        copies.append((part.at[t, edge_hi], lo_part.at[mt], (right, t)))
    copies = [
        remote(src, dst, send_rt.at[i], recv_rt.at[i], peer) for i, (src, dst, peer) in enumerate(copies)
    ]
    for copy in copies:
        copy.start()
    kept = pltpu.make_async_copy(part.at[mt], own_part.at[mt], local_sem.at[0])
    kept.start()
    target = jnp.where(
        pob < low,
        half - low + pob,
        jnp.where(pob >= count - high, half + rows + pob - (count - high), half + below + pob - low),
    )
    chooser = (target == lax.broadcasted_iota(jnp.int32, (2 * rows, 1), 0)).astype(f32)
    sizes = jnp.maximum(jnp.sum(chooser, axis=1, keepdims=True), 1.0)
    kept.wait()
    for copy in copies:
        copy.wait()

    def over_tp(ref):
        value = ref[0].astype(f32)
        for i in range(1, tp):
            value = value + ref[i].astype(f32)
        return value

    returned = jnp.concatenate([over_tp(lo_part), over_tp(own_part), over_tp(hi_part)], axis=0)
    shares = (returned.astype(bf).astype(f32) / sizes).astype(bf)
    grad_ref[...] = lax.dot_general(
        chooser.astype(bf), shares, over_first, preferred_element_type=f32
    ).astype(bf)


def shards(byte_states, patch_of_byte, patch_first, moved, w_qkv, d_attn):
    n, tp = lax.axis_size("ctx"), lax.axis_size("tp")
    rows, feats = d_attn.shape
    size, model = byte_states.shape
    heads = feats // HD
    groups = n // heads
    total = n * rows
    half = rows // 2
    width = model // tp
    block = 2 if heads % 2 == 0 else 1
    bf, f32 = jnp.bfloat16, jnp.float32
    dma = pltpu.SemaphoreType.DMA
    smem = pl.BlockSpec(memory_space=pltpu.SMEM)
    return tuple(pl.pallas_call(
        functools.partial(whole_kernel, n, tp, heads, rows, block),
        out_shape=[
            jax.ShapeDtypeStruct((rows, feats), bf),
            jax.ShapeDtypeStruct((size, width), bf),
        ],
        in_specs=[VM, VM, smem, smem, pl.BlockSpec(memory_space=pl.ANY), VM],
        out_specs=[VM] * 2,
        scratch_shapes=[
            pltpu.VMEM((2, half, model), bf), pltpu.VMEM((2, half, model), bf),
            pltpu.VMEM((rows, model), bf), pltpu.VMEM(w_qkv.shape, bf), pltpu.VMEM((3, rows, feats), bf),
            pltpu.VMEM((heads, rows, HD), bf), pltpu.VMEM((heads, rows, HD), bf),
            pltpu.VMEM((n, rows, HD), bf), pltpu.VMEM((n, rows, HD), bf),
            pltpu.VMEM((heads, rows, HD), bf), pltpu.VMEM((heads, rows, HD), bf),
            pltpu.VMEM((n, rows, HD), bf), pltpu.VMEM((n, rows, HD), bf),
            pltpu.VMEM((total, HD), f32), pltpu.VMEM((total, HD), f32),
            pltpu.VMEM((rows, feats), bf), pltpu.VMEM((rows, feats), bf),
            pltpu.VMEM((groups, rows, feats), bf), pltpu.VMEM((groups, rows, feats), bf),
            pltpu.VMEM((tp, rows, width), bf), pltpu.VMEM((tp, rows, width), bf),
            pltpu.VMEM((tp, half, width), bf), pltpu.VMEM((tp, half, width), bf),
            dma((3,)), dma((2,)), dma((2,)), dma((2, n)), dma((2, n)), dma((2, heads)), dma((2, heads)),
            dma((2, n)), dma((2, n)), dma((2, heads)), dma((2, heads)),
            dma((3 * tp - 1,)), dma((3 * tp - 1,)), dma((4,)),
        ],
        compiler_params=pltpu.CompilerParams(
            collective_id=0, has_side_effects=True, vmem_limit_bytes=56 << 20
        ),
        name="whole",
    )(byte_states, patch_of_byte.reshape(1, size), patch_first, moved, w_qkv, d_attn))


def solution(mesh):
    placed = (P("ctx", None), P("ctx"), P(), P(), P(None, None, "tp"), P("ctx", "tp"))
    return jax.shard_map(
        shards,
        mesh=mesh,
        in_specs=placed,
        out_specs=(P("ctx", "tp"), P("ctx", "tp")),
        check_vma=False,
    )
```

time: 306 us -> 61.8 us (0.20)
  waiting for transfers between devices: 143 us -> 0 us
  blocking collectives: 79.7 us -> 0 us
  Pallas kernels: 0 us -> 57.8 us
  matrix products: 35.5 us -> 0 us
  between operations: 16.6 us -> 0.64 us
  starting transfers between devices: 11.3 us -> 0 us
  local copies, waits for them, and re-layouts: 13.3 us -> 3.24 us
  other arithmetic: 6.49 us -> 0 us
    all_gather x4 -> x0, waiting for transfers between devices: 136 us -> none  [the longest x1 59.7 us: shards(): lax.all_gather(keyed, 'ctx', axis=0, tiled=True)]
    all_gather x3 -> x0, blocking collectives: 79.7 us -> none  [the longest x1 38.9 us: shards(): lax.all_gather(delta, 'ctx', axis=0, tiled=True)]
    pallas_call x0 -> x1, Pallas kernels: none -> 57.8 us  [shards(): pl.pallas_call(functools.partial(whole_kernel, n, tp, heads, rows, block)...]
    dot_general x15 -> x0, matrix products: 35.5 us -> none  [the longest x1 4.01 us: shards(): jnp.einsum('hqk,khd->qhd', dscore, keys3, preferred_element_type=jnp.floa...]
    ppermute x4 -> x0, starting transfers between devices: 11.1 us -> none  [the longest x2 8.48 us: extended_2(): before = lax.ppermute(last, axis, up)]
    dynamic_slice x6 -> x0, local copies, waits for them, and re-layouts: 4.28 us -> none  [pick_own(): return lax.dynamic_index_in_dim(values, index, 0, keepdims=False)]
    ppermute x4 -> x0, waiting for transfers between devices: 4.18 us -> none  [the longest x2 4.17 us: extended_2(): after = lax.ppermute(first, axis, down)]
  transfers between devices with their start and end apart: 9 -> 0, of which waited for: 6 -> 0; matrix products, arithmetic and copies ran while one was open for 11% -> 0% of each run, Pallas kernels for 0% -> 0%
where the time goes in v2:
time: 61.8 us; the launch traced here: 61.7 us
  Pallas kernels  57.8 us (94%)
  local copies, waits for them, and re-layouts  3.24 us (5%)
  between operations  0.64 us (1%)
    pallas_call x1, Pallas kernels, shards(): pl.pallas_call(functools.partial(whole_kernel, n, tp, heads, rows, block)...  57.8 us
    unnamed x2, local copies, waits for them, and re-layouts  3.24 us

profile of v2, /device:TPU:0, one launch (start us, length us, event | category | flops | bytes accessed | tf_op | source)
XLA Modules:
  0.0 61.7 jit_solution(16348588170209433723)
XLA Ops:
  0.6 57.8 %whole.1 = (bf16[64,1024]{1,0:T(8,128)(2,1)}, bf16[256,512]{1,0:T(8,128)(2,1)}) custom-call(bf16[256,1024]{1,0:T(8,128)(2,1)} %bytes_ref.1, s32[1,256]{1,0:T(1,128)} %bitcast.1, s32[16]{0:T(128)} %first_ref.1, s32[2,16]{1,0:T(2,128)} %moved_ref.1, bf16[3,1024,1024]{2,1,0:T(8,128)(2,1)} %w_ref.1, bf16[64,1024]{1,0:T(8,128)(2,1)} %d_ref.1), custom_call_target="tpu_custom_call" | custom-call | tf_op jit(solution)/shard_map/whole/pallas_call | solution.py:317
  58.4 1.6 %copy.10 = bf16[64,1024]{1,0:T(8,128)(2,1)} copy(bf16[64,1024]{1,0:T(8,128)(2,1)} %get-tuple-element.4) | data formatting | bytes 262144
  60.0 1.7 %copy.11 = bf16[256,512]{1,0:T(8,128)(2,1)} copy(bf16[256,512]{1,0:T(8,128)(2,1)} %get-tuple-element.5) | data formatting | bytes 524288

commit v3 on v2

--- a/solution.py
+++ b/solution.py
@@ -199,10 +199,17 @@
     back_o, back_q = back_mate(0, ob, o_in), back_mate(1, dqb, dq_in)
     row = lax.broadcasted_iota(jnp.int32, (rows, 1), 0)
     step_keys = 128 // rows if rows < 128 else 1
-    for b in range(heads // block):
+    send_dk, send_dv = back_peer(0, dkb, dk_in), back_peer(1, dvb, dv_in)
+
+    def reach_of(b):
+        if b < 0:
+            return 0
+        reach = min(n, (b + 1) * block * groups + 1)
+        return min(n, -(-reach // step_keys) * step_keys)
+
+    for b in reversed(range(heads // block)):
         lo = b * block
-        reach = min(n, (lo + block) * groups + 1)
-        reach = min(n, -(-reach // step_keys) * step_keys)
+        reach, settled = reach_of(b), reach_of(b - 1)
         keys = reach * rows
         q = qb[pl.ds(lo, block)].reshape(block * rows, HD)
         g = gb[pl.ds(lo, block)].reshape(block * rows, HD)
@@ -233,11 +240,24 @@
                 back_o(i).start()
                 back_q(i).start()
 
-    send_dk, send_dv = back_peer(0, dkb, dk_in), back_peer(1, dvb, dv_in)
-    dvb[...] = dva[...].astype(bf).reshape(n, rows, HD)
-    over_peers(send_dv)
-    dkb[...] = (dka[...] * scale).astype(bf).reshape(n, rows, HD)
-    over_peers(send_dk)
+        if reach > settled:
+            span = pl.ds(settled * rows, (reach - settled) * rows)
+            shape = (reach - settled, rows, HD)
+            dvb[pl.ds(settled, reach - settled)] = dva[span].astype(bf).reshape(shape)
+            dkb[pl.ds(settled, reach - settled)] = (dka[span] * scale).astype(bf).reshape(shape)
+
+            def send_back(peer, carry):
+                i = lax.rem(peer - me + n, n)
+
+                @pl.when(i != 0)
+                def _():
+                    send_dv(i).start()
+                    send_dk(i).start()
+
+                return carry
+
+            lax.fori_loop(settled, reach, send_back, 0)
+
     own = [
         pltpu.make_async_copy(src, dst, local_sem.at[i])
         for i, (src, dst) in enumerate((

time: 61.8 us -> 60.5 us (0.979)
  Pallas kernels: 57.8 us -> 56.3 us
    pallas_call x1, Pallas kernels: 57.8 us -> 56.3 us  [shards(): pl.pallas_call(functools.partial(whole_kernel, n, tp, heads, rows, block)...]
where the time goes in v3:
time: 60.5 us; the launch traced here: 60.2 us
  Pallas kernels  56.3 us (93%)
  local copies, waits for them, and re-layouts  3.24 us (5%)
  between operations  0.64 us (1%)
    pallas_call x1, Pallas kernels, shards(): pl.pallas_call(functools.partial(whole_kernel, n, tp, heads, rows, block)...  56.3 us
    unnamed x2, local copies, waits for them, and re-layouts  3.24 us

profile of v3, /device:TPU:0, one launch (start us, length us, event | category | flops | bytes accessed | tf_op | source)
XLA Modules:
  0.0 60.2 jit_solution(15027224418949451238)
XLA Ops:
  0.6 56.3 %whole.1 = (bf16[64,1024]{1,0:T(8,128)(2,1)}, bf16[256,512]{1,0:T(8,128)(2,1)}) custom-call(bf16[256,1024]{1,0:T(8,128)(2,1)} %bytes_ref.1, s32[1,256]{1,0:T(1,128)} %bitcast.1, s32[16]{0:T(128)} %first_ref.1, s32[2,16]{1,0:T(2,128)} %moved_ref.1, bf16[3,1024,1024]{2,1,0:T(8,128)(2,1)} %w_ref.1, bf16[64,1024]{1,0:T(8,128)(2,1)} %d_ref.1), custom_call_target="tpu_custom_call" | custom-call | tf_op jit(solution)/shard_map/whole/pallas_call | solution.py:337
  56.9 1.6 %copy.10 = bf16[64,1024]{1,0:T(8,128)(2,1)} copy(bf16[64,1024]{1,0:T(8,128)(2,1)} %get-tuple-element.4) | data formatting | bytes 262144
  58.5 1.7 %copy.11 = bf16[256,512]{1,0:T(8,128)(2,1)} copy(bf16[256,512]{1,0:T(8,128)(2,1)} %get-tuple-element.5) | data formatting | bytes 524288
